TPU v7x, 128 devices: a whole 4x4x4 slice. The times are simulated.
128 devices in a mesh: row: 8 (over x, core), col: 16 (over z, y).
Axes of the slice: x: 4, y: 4, z: 4, core: 2. Of those that a mesh axis runs over, the one named last changes fastest.
Arguments:
- stored: float32 [16384, 16384], P('row', 'col'), as said below
Outputs:
- updated: float32 [16384, 16384], P('row', 'col')
- log_det: float32 [], replicated
Inputs may be any that keep to these rules, and one draw needn't show every extreme that they name: `stored`: read back into global order, the matrix is symmetric positive definite, with every eigenvalue at least 1.
All inputs are finite; a program needn't handle non-finite values.
Results may differ from a plain program's by a relative error of at most 0.0001.
Values sent between devices are 32-bit elements; how exact they have to be, the bound alone decides.
A program may use at most 256 MiB of HBM per device.

v0:
```python
import jax
import jax.numpy as jnp
from jax import lax
from jax.sharding import PartitionSpec as P

NB = 512
PANELS = 2


def from_root(value, axis, root):
    return lax.dynamic_index_in_dim(lax.all_gather(value, axis), root, 0, keepdims=False)


def from_root_2(value, axis, source):
    kept = jnp.where(lax.axis_index(axis) == source, value, 0).astype(value.dtype)
    return lax.psum(kept, axis)


def per_device(stored):
    row_count = lax.axis_size("row")
    col_count = lax.axis_size("col")
    row_index = lax.axis_index("row")
    col_index = lax.axis_index("col")
    local_rows, local_cols = stored.shape
    ratio = col_count // row_count
    col_blocks = local_cols // NB
    row_block = jnp.arange(local_rows, dtype=jnp.int32) // NB * row_count + row_index
    col_block = jnp.arange(local_cols, dtype=jnp.int32) // NB * col_count + col_index
    identity = jnp.eye(NB, dtype=jnp.float32)
    matrix = stored
    log_total = jnp.zeros((), jnp.float32)
    for number in range(PANELS):
        own_col = number // col_count
        own_row = number // row_count
        root_row = number % row_count
        root_col = number % col_count
        column_slab = matrix[:, own_col * NB : (own_col + 1) * NB]
        pivot_block = column_slab[own_row * NB : (own_row + 1) * NB]
        pivot_block = from_root(pivot_block, "row", root_row)
        factor = jnp.linalg.cholesky(pivot_block)
        inverse = jax.scipy.linalg.solve_triangular(factor, identity, lower=True)
        solved = jnp.dot(
            column_slab,
            inverse.T,
            precision=lax.Precision.HIGHEST,
            preferred_element_type=jnp.float32,
        )
        below_mask = (row_block > number)[:, None]
        at_mask = (row_block == number)[:, None]
        tiled = jnp.tile(factor, (local_rows // NB, 1))
        panel_full = jnp.where(below_mask, solved, jnp.where(at_mask, tiled, 0.0))
        log_term = 2.0 * jnp.sum(jnp.log(jnp.diagonal(factor)))
        panel_full = from_root_2(panel_full, "col", root_col)
        log_total = log_total + jnp.where(col_index == root_col, log_term, 0.0)
        picked = lax.dynamic_index_in_dim(
            panel_full.reshape(col_blocks, ratio, NB, NB), col_index // row_count, 1, keepdims=False
        )
        right_rows = from_root_2(picked.reshape(local_cols, NB), "row", col_index % row_count)
        left_rows = jnp.where(below_mask, panel_full, 0.0)
        right_rows = jnp.where((col_block > number)[:, None], right_rows, 0.0)
        matrix = matrix - jnp.dot(
            left_rows,
            right_rows.T,
            precision=lax.Precision.HIGHEST,
            preferred_element_type=jnp.float32,
        )
        old_column = matrix[:, own_col * NB : (own_col + 1) * NB]
        new_column = jnp.where(col_index == root_col, panel_full, old_column)
        matrix = matrix.at[:, own_col * NB : (own_col + 1) * NB].set(new_column)
        upper_mask = at_mask & (col_block > number)[None, :]
        matrix = jnp.where(upper_mask, 0.0, matrix)
    log_total = lax.psum(log_total, "col")
    return (matrix, log_total)


def solution(mesh):
    placed = (P("row", "col"),)
    return jax.shard_map(
        per_device, mesh=mesh, in_specs=placed, out_specs=(P("row", "col"), P()), check_vma=False
    )
```

profile of v0, /device:TPU:64, one launch (start us, length us, event | category | flops | bytes accessed | tf_op | source)
XLA Modules:
  0.0 887.2 jit_solution(12284626979522440874)
XLA Ops:
  7.2 9.1 %copy.16 = f32[2048,1024]{0,1:T(8,128)} copy(f32[2048,1024]{1,0:T(8,128)} %param.8) | data formatting | bytes 16777216 | tf_op args[0]
  16.3 2.4 slice.161
  18.9 51.2 %all-gather.5.cloned.1.call-done = f32[4096,512]{0,1:T(8,128)} async-done(((f32[512,512]{0,1:T(8,128)}), f32[4096,512]{0,1:T(8,128)}) %all-gather.5.cloned.1.call-update) | async-done | bytes 8388624 | tf_op jit(solution)/shard_map/all_gather | solution.py:11
  73.3 11.7 %cholesky.286 = f32[128,128]{1,0:T(8,128)S(1)} custom-call(f32[128,128]{1,0:T(8,128)S(1)} %cholesky.426), custom_call_target="Cholesky" | custom-call | tf_op jit(solution)/shard_map/jit(cholesky)/cholesky | solution.py:40
  85.0 9.8 %custom-call.31 = f32[1,128,128]{1,2,0:T(8,128)S(1)} custom-call(f32[1,128,128]{2,1,0:T(8,128)S(1)} %get-tuple-element.91), custom_call_target="InvertDiagBlocksLowerTriangular" | custom-call | tf_op jit(solution)/shard_map/jit(cholesky)/cholesky | solution.py:40
  97.5 11.7 %cholesky.305 = f32[128,128]{1,0:T(8,128)S(1)} custom-call(f32[128,128]{1,0:T(8,128)S(1)} %cholesky.430), custom_call_target="Cholesky" | custom-call | tf_op jit(solution)/shard_map/jit(cholesky)/cholesky | solution.py:40
  109.2 10.2 %custom-call.32 = f32[1,128,128]{1,2,0:T(8,128)S(1)} custom-call(f32[1,128,128]{2,1,0:T(8,128)S(1)} %get-tuple-element.88), custom_call_target="InvertDiagBlocksLowerTriangular" | custom-call | tf_op jit(solution)/shard_map/jit(cholesky)/cholesky | solution.py:40
  121.1 11.7 %cholesky.326 = f32[128,128]{1,0:T(8,128)S(1)} custom-call(f32[128,128]{1,0:T(8,128)S(1)} %cholesky.435), custom_call_target="Cholesky" | custom-call | tf_op jit(solution)/shard_map/jit(cholesky)/cholesky | solution.py:40
  133.5 9.8 %custom-call.33 = f32[1,128,128]{1,2,0:T(8,128)S(1)} custom-call(f32[1,128,128]{2,1,0:T(8,128)S(1)} %get-tuple-element.85), custom_call_target="InvertDiagBlocksLowerTriangular" | custom-call | tf_op jit(solution)/shard_map/jit(cholesky)/cholesky | solution.py:40
  144.8 11.7 %cholesky.343 = f32[128,128]{1,0:T(8,128)S(1)} custom-call(f32[128,128]{1,0:T(8,128)S(1)} %convolution_subtract_fusion.11), custom_call_target="Cholesky" | custom-call | tf_op jit(solution)/shard_map/jit(cholesky)/cholesky | solution.py:40
  161.8 12.0 %while.6 = (s32[]{:T(128)}, f32[512,512]{1,0:T(8,128)}, s32[4,2]{0,1:T(2,128)S(1)}, f32[4,128,128]{2,1,0:T(8,128)S(1)}, s32[]{:T(128)}) while((s32[]{:T(128)}, f32[512,512]{1,0:T(8,128)}, s32[4,2]{0,1:T(2,128)S(1)}, f32[4,128,128]{2,1,0:T(8,128)S(1)}, s32[]{:T(128)}) %tuple.69), condition=%wide.while_cond.2, body=%wide.while_body.2.sunk | while | flops 2 | bytes 131189 | solution.py:41
  162.5 2.3 bitcast_dynamic-update-slice_fusion.4
  165.5 2.3 bitcast_dynamic-update-slice_fusion.4
  168.5 2.3 bitcast_dynamic-update-slice_fusion.4
  171.6 2.3 bitcast_dynamic-update-slice_fusion.4
  173.8 39.3 %custom-call.34 = f32[4,128,128]{1,2,0:T(8,128)S(1)} custom-call(f32[4,128,128]{2,1,0:T(8,128)S(1)} %get-tuple-element.42), custom_call_target="InvertDiagBlocksLowerTriangular" | custom-call | tf_op jit(solution)/shard_map/jit(_solve_triangular)/triangular_solve | solution.py:41
  223.5 8.5 fusion.4
  232.5 103.4 %all-reduce.6.cloned.1.call-done = f32[2048,512]{0,1:T(8,128)} async-done(((f32[2048,512]{0,1:T(8,128)}), f32[2048,512]{0,1:T(8,128)}) %all-reduce.6.cloned.1.call-update) | async-done | bytes 4194320 | tf_op jit(solution)/shard_map/psum | solution.py:16
  335.9 6.6 reshape.171
  342.5 9.4 %fusion.21 = f32[2,512,512]{1,0,2:T(2,128)S(1)} fusion(pred[]{:T(512)S(6)} %eq.40, f32[2,2,512,512]{2,1,0,3:T(2,128)} %reshape.171, s32[]{:T(128)S(6)} %select_n.161), kind=kLoop, calls=%fused_computation.27 | loop fusion | flops 524288 | bytes 4194309 | tf_op jit(solution)/shard_map/jit(_where)/select_n | solution.py:15
  354.5 64.9 %all-reduce.8.cloned.1.call-done = f32[1024,512]{0,1:T(8,128)} async-done(((f32[1024,512]{0,1:T(8,128)}), f32[1024,512]{0,1:T(8,128)}) %all-reduce.8.cloned.1.call-update) | async-done | bytes 2097168 | tf_op jit(solution)/shard_map/psum | solution.py:16
  419.4 17.1 %fusion.11 = f32[2048,1024]{0,1:T(8,128)S(1)} fusion(f32[2048,1024]{0,1:T(8,128)} %copy.16, f32[2048,512]{0,1:T(8,128)} %all-reduce.6.cloned.1.call-done, f32[1024,512]{0,1:T(8,128)} %all-reduce.8.cloned.1.call-done, pred[2048]{0:T(1024)(128)(4,1)S(1)} %get-tuple-element.100, pred[1024]{0:T(1024)(128)(4,1)S(1)} %fusion.120), kind=kOutput, calls=%fused_computation.25 | convolution fusion | flops 12888571904 | bytes 23071744 | tf_op jit(solution)/shard_map/dot_general | solution.py:61
  439.4 3.4 copy-done
  444.3 49.2 %all-gather.7.cloned.1.call-done = f32[4096,512]{0,1:T(8,128)} async-done(((f32[512,512]{0,1:T(8,128)}), f32[4096,512]{0,1:T(8,128)}) %all-gather.7.cloned.1.call-update) | async-done | bytes 8388624 | tf_op jit(solution)/shard_map/all_gather | solution.py:11
  493.4 2.4 slice.166
  499.8 11.7 %cholesky.358 = f32[128,128]{1,0:T(8,128)S(1)} custom-call(f32[128,128]{1,0:T(8,128)S(1)} %cholesky.439), custom_call_target="Cholesky" | custom-call | tf_op jit(solution)/shard_map/jit(cholesky)/cholesky | solution.py:40
  512.2 9.8 %custom-call.35 = f32[1,128,128]{1,2,0:T(8,128)S(1)} custom-call(f32[1,128,128]{2,1,0:T(8,128)S(1)} %get-tuple-element.81), custom_call_target="InvertDiagBlocksLowerTriangular" | custom-call | tf_op jit(solution)/shard_map/jit(cholesky)/cholesky | solution.py:40
  524.7 11.7 %cholesky.377 = f32[128,128]{1,0:T(8,128)S(1)} custom-call(f32[128,128]{1,0:T(8,128)S(1)} %cholesky.443), custom_call_target="Cholesky" | custom-call | tf_op jit(solution)/shard_map/jit(cholesky)/cholesky | solution.py:40
  537.1 10.0 %custom-call.36 = f32[1,128,128]{1,2,0:T(8,128)S(1)} custom-call(f32[1,128,128]{2,1,0:T(8,128)S(1)} %get-tuple-element.78), custom_call_target="InvertDiagBlocksLowerTriangular" | custom-call | tf_op jit(solution)/shard_map/jit(cholesky)/cholesky | solution.py:40
  548.6 11.7 %cholesky.398 = f32[128,128]{1,0:T(8,128)S(1)} custom-call(f32[128,128]{1,0:T(8,128)S(1)} %cholesky.448), custom_call_target="Cholesky" | custom-call | tf_op jit(solution)/shard_map/jit(cholesky)/cholesky | solution.py:40
  561.0 9.8 %custom-call.37 = f32[1,128,128]{1,2,0:T(8,128)S(1)} custom-call(f32[1,128,128]{2,1,0:T(8,128)S(1)} %get-tuple-element.75), custom_call_target="InvertDiagBlocksLowerTriangular" | custom-call | tf_op jit(solution)/shard_map/jit(cholesky)/cholesky | solution.py:40
  572.3 11.7 %cholesky.415 = f32[128,128]{1,0:T(8,128)S(1)} custom-call(f32[128,128]{1,0:T(8,128)S(1)} %convolution_subtract_fusion.10), custom_call_target="Cholesky" | custom-call | tf_op jit(solution)/shard_map/jit(cholesky)/cholesky | solution.py:40
  590.3 11.5 %while.7 = (s32[]{:T(128)}, f32[512,512]{1,0:T(8,128)}, s32[4,2]{0,1:T(2,128)S(1)}, f32[4,128,128]{2,1,0:T(8,128)S(1)}, s32[]{:T(128)}) while((s32[]{:T(128)}, f32[512,512]{1,0:T(8,128)}, s32[4,2]{0,1:T(2,128)S(1)}, f32[4,128,128]{2,1,0:T(8,128)S(1)}, s32[]{:T(128)}) %tuple.87), condition=%wide.while_cond.2.clone, body=%wide.while_body.2.clone.sunk | while | flops 2 | bytes 131189 | solution.py:41
  590.9 2.3 bitcast_dynamic-update-slice_fusion.5
  593.8 2.3 bitcast_dynamic-update-slice_fusion.5
  596.6 2.3 bitcast_dynamic-update-slice_fusion.5
  602.5 40.1 %custom-call.38 = f32[4,128,128]{1,2,0:T(8,128)S(1)} custom-call(f32[4,128,128]{2,1,0:T(8,128)} %copy-done.8), custom_call_target="InvertDiagBlocksLowerTriangular" | custom-call | tf_op jit(solution)/shard_map/jit(_solve_triangular)/triangular_solve | solution.py:41
  651.5 8.5 select_select_fusion.2
  660.3 103.6 %all-reduce.10.cloned.1.call-done = f32[2048,512]{0,1:T(8,128)} async-done(((f32[2048,512]{0,1:T(8,128)}), f32[2048,512]{0,1:T(8,128)}) %all-reduce.10.cloned.1.call-update) | async-done | bytes 4194320 | tf_op jit(solution)/shard_map/psum | solution.py:16
  764.0 6.6 reshape.172
  770.5 9.4 %fusion.22 = f32[2,512,512]{1,0,2:T(2,128)S(1)} fusion(pred[]{:T(512)S(6)} %eq.40, f32[2,2,512,512]{2,1,0,3:T(2,128)} %reshape.172, s32[]{:T(128)S(6)} %select_n.161), kind=kLoop, calls=%fused_computation.28 | loop fusion | flops 524288 | bytes 4194309 | tf_op jit(solution)/shard_map/jit(_where)/select_n | solution.py:15
  781.8 4.5 gather_fusion
  787.6 4.5 gather_fusion.1
  793.4 33.0 %psum.39 = f32[]{:T(128)} all-reduce(f32[]{:T(128)S(6)} %add.143), channel_id=1, replica_groups=mesh['row'=8,'col'=16] {'col'}, use_global_device_ids=true, to_apply=%region_15.18 | all-reduce | flops 1 | bytes 8 | tf_op jit(solution)/shard_map/psum | solution.py:72
  826.4 21.3 %all-reduce.12.cloned.1.call-done = f32[1024,512]{0,1:T(8,128)} async-done(((f32[1024,512]{0,1:T(8,128)}), f32[1024,512]{0,1:T(8,128)}) %all-reduce.12.cloned.1.call-update) | async-done | bytes 2097168 | tf_op jit(solution)/shard_map/psum | solution.py:16
  847.7 17.1 %fusion.14 = f32[2048,1024]{0,1:T(8,128)S(1)} fusion(f32[2048,1024]{0,1:T(8,128)} %copy-done, f32[2048,512]{0,1:T(8,128)} %all-reduce.10.cloned.1.call-done, f32[1024,512]{0,1:T(8,128)} %all-reduce.12.cloned.1.call-done, pred[2048]{0:T(1024)(128)(4,1)S(1)} %get-tuple-element.98, pred[1024]{0:T(1024)(128)(4,1)S(1)} %fusion.121), kind=kOutput, calls=%fused_computation.26 | convolution fusion | flops 12888571904 | bytes 23071744 | tf_op jit(solution)/shard_map/dot_general | solution.py:61
  866.8 4.1 and_select_fusion.1
  870.9 9.2 %copy.22 = f32[2048,1024]{1,0:T(8,128)} copy(f32[2048,1024]{0,1:T(8,128)} %and_select_fusion.1) | data formatting | bytes 16777216
  (137 shorter events, 67.3 us)
Async XLA Ops:
  7.2 63.0 %all-gather.5.cloned.1.call-start = ((), (), s32[]{:S(2)}) async-start(), calls=%async_computation.4 | async-start | bytes 9437184 | tf_op jit(solution)/shard_map/all_gather | solution.py:11
  18.7 317.2 %all-reduce.6.cloned.1.call-start = ((), (), s32[]{:S(2)}) async-start(), calls=%async_computation | async-start | bytes 8388608 | tf_op jit(solution)/shard_map/psum | solution.py:16
  73.2 11.8 %copy-start.7 = (f32[512,512]{1,0:T(8,128)}, f32[512,512]{1,0:T(8,128)S(1)}, u32[]{:S(2)}) copy-start(f32[512,512]{1,0:T(8,128)S(1)} %fusion.44) | copy-start | bytes 3145732
  214.5 6.0 copy-start.5
  218.4 4.9 slice-start.2
  221.3 2.2 slice-start.3
  232.0 187.4 %all-reduce.8.cloned.1.call-start = ((), (), s32[]{:S(2)}) async-start(), calls=%async_computation.1 | async-start | bytes 4194304 | tf_op jit(solution)/shard_map/psum | solution.py:16
  353.7 139.7 %all-gather.7.cloned.1.call-start = ((), (), s32[]{:S(2)}) async-start(), calls=%async_computation.5 | async-start | bytes 9437184 | tf_op jit(solution)/shard_map/all_gather | solution.py:11
  419.4 17.2 %copy-start.1 = (f32[2048,512]{0,1:T(8,128)S(1)}, f32[2048,512]{0,1:T(8,128)}, u32[]{:S(2)}) copy-start(f32[2048,512]{0,1:T(8,128)} %all-reduce.6.cloned.1.call-done) | copy-start | bytes 12582916
  439.4 3.4 copy-start
  444.0 319.9 %all-reduce.10.cloned.1.call-start = ((), (), s32[]{:S(2)}) async-start(), calls=%async_computation.2 | async-start | bytes 8388608 | tf_op jit(solution)/shard_map/psum | solution.py:16
  498.8 1.0 copy-start.6
  584.0 3.7 copy-start.3
  601.7 0.7 copy-start.8
  642.6 6.0 copy-start.4
  646.4 4.9 slice-start
  649.3 2.2 slice-start.1
  660.1 187.6 %all-reduce.12.cloned.1.call-start = ((), (), s32[]{:S(2)}) async-start(), calls=%async_computation.3 | async-start | bytes 4194304 | tf_op jit(solution)/shard_map/psum | solution.py:16
  847.7 17.2 %copy-start.2 = (f32[2048,512]{0,1:T(8,128)S(1)}, f32[2048,512]{0,1:T(8,128)}, u32[]{:S(2)}) copy-start(f32[2048,512]{0,1:T(8,128)} %all-reduce.10.cloned.1.call-done) | copy-start | bytes 12582916
Sparse Core Ops, SparseCore 0:
  18.9 51.2 all-gather.4
  232.1 103.7 all-reduce.5
  353.8 65.5 all-reduce.7
  444.1 49.2 all-gather.6
  660.2 103.6 all-reduce.9
  781.9 65.7 all-reduce.11
where the time goes:
time: 899 us; the launch traced here: 887 us
  waiting for transfers between devices  394 us (44%)
  other arithmetic  273 us (30%)
  local copies, waits for them, and re-layouts  90.5 us (10%)
  matrix products  74.1 us (8%)
  blocking collectives  33 us (4%)
  between operations  21.5 us (2%)
    psum x4, waiting for transfers between devices, from_root_2(): return lax.psum(kept, axis)  293 us
    another operation x29, other arithmetic, per_device(): factor = jnp.linalg.cholesky(pivot_block)  159 us
    all_gather x2, waiting for transfers between devices, from_root(): lax.all_gather(value, axis)  100 us
    another operation x5, other arithmetic, per_device(): inverse = jax.scipy.linalg.solve_triangular(factor, identity, lower=True)  81.7 us
    dot_general x2, matrix products, per_device(): jnp.dot(left_rows, right_rows.T, precision=lax.Precision.HIGHEST, preferr...  34.3 us
    psum x1, blocking collectives, per_device(): log_total = lax.psum(log_total, 'col')  33 us
    unnamed x32, local copies, waits for them, and re-layouts  31.5 us
    another operation x27, local copies, waits for them, and re-layouts, per_device(): inverse = jax.scipy.linalg.solve_triangular(factor, identity, lower=True)  23.4 us
  transfers between devices with their start and end apart: 6, of which 6 were waited for; matrix products, arithmetic and copies ran while one was open for 1% of the time, Pallas kernels for 0%

commit v1 on v0

v1 whole, which is shorter than its diff:
```python
import jax
import jax.numpy as jnp
from jax import lax
from jax.experimental import pallas as pl
from jax.experimental.pallas import tpu as pltpu
from jax.sharding import PartitionSpec as P

NB = 512
TB = 128
CH = 32
F32 = jnp.float32
BF = jnp.bfloat16
HI = lax.Precision.HIGHEST
MESH = pl.DeviceIdType.MESH

TREES = (
    (1, 27, 41, 48, 48, 39, 49, 64, 64, 53, 65, 80, 48, 36, 49, 64),
    (2, 48, 64, 48, 23, 40, 58, 46, 35, 50, 66, 50, 48, 64, 80, 64),
    (4, 48, 38, 30, 48, 64, 52, 33, 64, 80, 68, 53, 48, 64, 52, 45),
    (8, 48, 64, 48, 48, 64, 80, 64, 44, 56, 72, 56, 29, 43, 58, 34),
)
MAXDEPTH = 5
SKEW = 2
NX = 16
ND = 4
NA = 16
LAG = 5 + 3 * SKEW


def lookup(table, position):
    value = jnp.int32(table[0])
    for index in range(1, len(table)):
        value = jnp.where(position == index, jnp.int32(table[index]), value)
    return value


def comm_kernel(stored, arow_out, acol_out, diag_out, arow, acol, diag,
                lsem, x_recv, xp_recv, x_send, xp_send, p_recv, p_send, d_recv, d_send):
    row = lax.axis_index("row")
    col = lax.axis_index("col")
    x, core = row // 2, row % 2
    z, y = col // 4, col % 4
    partner = (x * 2 + (1 - core), col)
    x_next = (((x + 1) % 4) * 2 + core, col)
    x_prev = (((x + 3) % 4) * 2 + core, col)
    plane = (
        (row, z * 4 + (y + 1) % 4),
        (row, ((z + 1) % 4) * 4 + y),
        (row, z * 4 + (y + 3) % 4),
        (row, ((z + 3) % 4) * 4 + y),
    )
    barrier = pltpu.get_barrier_semaphore()
    for other in (partner, x_next, x_prev) + plane:
        pl.semaphore_signal(barrier, inc=1, device_id=other, device_id_type=MESH)

    @pl.when(x == 0)
    def _():
        own = pltpu.make_async_copy(stored.at[pl.ds(0, NB), :], acol.at[core], lsem.at[0])
        own.start()
        own.wait()

    for k in range(2):
        @pl.when(col == k)
        def _():
            own = pltpu.make_async_copy(stored.at[:, pl.ds(0, NB)], arow.at[k], lsem.at[1])
            own.start()
            own.wait()

    pl.semaphore_wait(barrier, 7)

    def x_view(which, d, i):
        rows = pl.multiple_of((2 * (i % 8) + d) * CH, CH)
        return acol.at[which, pl.ds(rows, CH), pl.ds(pl.multiple_of((i // 8) * NB, NB), NB)]

    def x_copy(d, i):
        view = x_view(core, d, i)
        return pltpu.make_async_remote_copy(
            view, view, x_send.at[d], x_recv.at[d, i], device_id=(x_next, x_prev)[d], device_id_type=MESH)

    def xp_copy(d, i, which):
        view = x_view(which, d, i)
        return pltpu.make_async_remote_copy(
            view, view, xp_send.at[d], xp_recv.at[d, i], device_id=partner, device_id_type=MESH)

    def p_view(k, t, j):
        rows = pl.multiple_of((4 * (j - ND) + t) * CH, CH)
        return arow.at[k, pl.ds(rows, CH), :]

    def d_view(slot, t, j):
        return diag.at[slot, pl.ds(pl.multiple_of((4 * j + t) * CH, CH), CH), :]

    def d_source(which, t, j):
        return acol.at[which, pl.ds(pl.multiple_of((4 * j + t) * CH, CH), CH), pl.ds(0, NB)]

    def p_copy(src, dst, k, t, j, way):
        return pltpu.make_async_remote_copy(
            src, dst, p_send.at[k, t, way], p_recv.at[k, t, j], device_id=plane[way], device_id_type=MESH)

    def d_copy(slot, k, t, j):
        view = d_view(slot, t, j)
        return pltpu.make_async_remote_copy(
            view, view, d_send.at[k, t], d_recv.at[k, t, j], device_id=partner, device_id_type=MESH)

    codes = []
    for k in range(2):
        position = z * 4 + (y + 4 - k) % 4
        codes.append([lookup(TREES[t], position) for t in range(4)])
    steps = LAG + ND + NA + SKEW * MAXDEPTH

    def step(s, _):
        for d in range(2):
            distance = x if d == 0 else (4 - x) % 4
            i = s - SKEW * distance

            @pl.when((i >= 0) & (i < NX))
            def _():
                @pl.when(distance > 0)
                def _():
                    x_copy(d, i).wait_recv()

                @pl.when(i > 0)
                def _():
                    xp_copy(d, i - 1, core).wait_send()

                @pl.when((i > 0) & (distance < 3))
                def _():
                    x_copy(d, i - 1).wait_send()

                @pl.when(distance < 3)
                def _():
                    x_copy(d, i).start()

                xp_copy(d, i, core).start()

            h = i - SKEW

            @pl.when((h >= 0) & (h < NX))
            def _():
                xp_copy(d, h, 1 - core).wait_recv()

        for k in range(2):
            slot = core + k
            has_diag = (core == 0) if k == 0 else (core >= 0)
            for t in range(4):
                depth = codes[k][t] // 16
                mask = codes[k][t] % 16
                j = s - LAG - SKEW * depth
                in_diag = (j >= 0) & (j < ND) & has_diag
                in_rows = (j >= ND) & (j < ND + NA)
                active = in_diag | in_rows
                started = (j > 0) & active & ((j > ND) | has_diag)

                @pl.when(active & (depth > 0))
                def _():
                    p_copy(p_view(k, t, ND), p_view(k, t, ND), k, t, j, 0).wait_recv()

                for way in range(4):
                    child = (mask // (1 << way)) % 2 == 1

                    @pl.when(started & child)
                    def _():
                        p_copy(p_view(k, t, ND), p_view(k, t, ND), k, t, j - 1, way).wait_send()

                    @pl.when(in_rows & child)
                    def _():
                        p_copy(p_view(k, t, j), p_view(k, t, j), k, t, j, way).start()

                    @pl.when(in_diag & child & (depth == 0))
                    def _():
                        p_copy(d_source(core, t, j), d_view(slot, t, j), k, t, j, way).start()

                    @pl.when(in_diag & child & (depth > 0))
                    def _():
                        p_copy(d_view(slot, t, j), d_view(slot, t, j), k, t, j, way).start()

                @pl.when(in_diag & (depth > 0))
                def _():
                    @pl.when(j > 0)
                    def _():
                        d_copy(slot, k, t, j - 1).wait_send()
                    d_copy(slot, k, t, j).start()
        return 0

    lax.fori_loop(0, steps, step, 0)

    for d in range(2):
        distance = x if d == 0 else (4 - x) % 4
        xp_copy(d, NX - 1, core).wait_send()

        @pl.when(distance < 3)
        def _():
            x_copy(d, NX - 1).wait_send()
    for k in range(2):
        source = col == k
        away = col != k
        for t in range(4):
            mask = codes[k][t] % 16
            for way in range(4):
                @pl.when((mask // (1 << way)) % 2 == 1)
                def _():
                    p_copy(p_view(k, t, ND), p_view(k, t, ND), k, t, ND + NA - 1, way).wait_send()
            if k == 0:
                sends, gets = (core == 0) & away, (core == 1) & away
            else:
                sends, gets = away, away

            @pl.when(sends)
            def _():
                d_copy(0, k, t, 0).wait_send()

            @pl.when(gets)
            def _():
                for j in range(ND):
                    d_copy(0, k, t, j).wait_recv()

    @pl.when(col == 0)
    def _():
        diag[0] = acol[0, :, pl.ds(0, NB)]

    @pl.when(col == 1)
    def _():
        diag[1] = acol[0, :, pl.ds(0, NB)]
        diag[2] = acol[1, :, pl.ds(0, NB)]

    outs = [
        pltpu.make_async_copy(arow, arow_out, lsem.at[0]),
        pltpu.make_async_copy(acol, acol_out, lsem.at[1]),
    ]
    for copy in outs:
        copy.start()
    for copy in outs:
        copy.wait()
    last = pltpu.make_async_copy(diag, diag_out, lsem.at[2])
    last.start()
    last.wait()


def gather(stored):
    rows, cols = stored.shape
    shapes = ((2, rows, NB), (2, NB, cols), (3, NB, NB))
    dma = pltpu.SemaphoreType.DMA
    return pl.pallas_call(
        comm_kernel,
        name="gather_panels",
        out_shape=tuple(jax.ShapeDtypeStruct(s, F32) for s in shapes),
        in_specs=[pl.BlockSpec(memory_space=pl.ANY)],
        out_specs=(pl.BlockSpec(memory_space=pl.ANY),) * 3,
        scratch_shapes=[pltpu.VMEM(s, F32) for s in shapes]
        + [
            dma((3,)),
            dma((2, NX)),
            dma((2, NX)),
            dma((2,)),
            dma((2,)),
            dma((2, 4, ND + NA)),
            dma((2, 4, 4)),
            dma((2, 4, ND)),
            dma((2, 4)),
        ],
        compiler_params=pltpu.CompilerParams(
            collective_id=0, has_side_effects=True, vmem_limit_bytes=60 << 20),
    )(stored)


def spread(value, k):
    return jnp.broadcast_to(value[k : k + 1, :], (8, 128))


def split3(value):
    high = value.astype(BF)
    rest = value - high.astype(F32)
    middle = rest.astype(BF)
    low = (rest - middle.astype(F32)).astype(BF)
    return high, middle, low


def split2(value):
    high = value.astype(BF)
    return high, (value - high.astype(F32)).astype(BF)


def factor_tile(t, ld):
    sub = lax.broadcasted_iota(jnp.int32, (8, 128), 0)
    for p in range(8):
        r0 = 16 * p
        r = [[t[r0 + 8 * g : r0 + 8 * g + 8, 128 * h : 128 * h + 128] for h in range(2)] for g in range(2)]
        top = [jnp.broadcast_to(r[0][0][:, r0 + j : r0 + j + 1], (8, 128)) for j in range(8)]
        bot = [jnp.broadcast_to(r[1][0][:, r0 + j : r0 + j + 1], (8, 128)) for j in range(16)]
        piv = [jnp.ones((8, 128), F32), jnp.ones((8, 128), F32)]
        for k in range(16):
            g, kk = divmod(k, 8)
            pv = spread(top[k] if g == 0 else bot[k], kk)
            inv = 1.0 / pv
            piv[g] = jnp.where(sub == kk, pv, piv[g])
            mb = bot[k] * inv
            mt = top[k] * inv if g == 0 else None
            for j in range(k + 1, 16):
                s = spread(top[k], j) if j < 8 else spread(bot[k], j - 8)
                bot[j] = bot[j] - mb * s
                if j < 8:
                    top[j] = top[j] - mt * s
            for h in range(2):
                u = spread(r[g][h], kk)
                if g == 0:
                    r[0][h] = r[0][h] - jnp.where(sub > kk, mt, 0.0) * u
                    r[1][h] = r[1][h] - mb * u
                else:
                    r[1][h] = r[1][h] - jnp.where(sub > kk, mb, 0.0) * u
        ld[...] += jnp.log(piv[0]) + jnp.log(piv[1])
        rows = []
        for g in range(2):
            rs = lax.rsqrt(piv[g])
            rows.append([r[g][h] * rs for h in range(2)])
            for h in range(2):
                t[r0 + 8 * g : r0 + 8 * g + 8, 128 * h : 128 * h + 128] = rows[g][h]
        if p < 7:
            uh, um, ul = split3(jnp.concatenate([rows[0][0], rows[1][0]], 0))
            wh, wm, wl = split3(jnp.concatenate([rows[0][1], rows[1][1]], 0))
            lhs = jnp.concatenate([uh, uh, um, uh, ul, um], 0)
            rhs = jnp.concatenate(
                [jnp.concatenate([uh, um, uh, ul, uh, um], 0), jnp.concatenate([wh, wm, wh, wl, wh, wm], 0)], 1)
            upd = lax.dot_general(lhs, rhs, (((0,), (0,)), ((), ())), preferred_element_type=F32)
            t[r0 + 16 :, :] -= upd[r0 + 16 :, :]


def factor_block(b, t, ud, ld):
    ri = lax.broadcasted_iota(jnp.int32, (TB, TB), 0)
    ci = lax.broadcasted_iota(jnp.int32, (TB, TB), 1)
    n = NB // TB

    def step(blk, _):
        base = pl.multiple_of(blk * TB, TB)
        rows = pl.ds(base, TB)
        t[:, :TB] = b[rows, rows]
        t[:, TB:] = jnp.where(ri == ci, 1.0, 0.0)
        factor_tile(t, ld)
        w = jnp.where(ri >= ci, t[:, TB:], 0.0)
        ud[blk] = jnp.where(ri <= ci, t[:, :TB], 0.0)
        b[rows, :] = jnp.dot(w, b[rows, :], precision=HI, preferred_element_type=F32)
        b[rows, rows] = w

        def trail(i, _):
            ir = pl.ds(pl.multiple_of(i * TB, TB), TB)
            b[ir, rows] = jnp.zeros((TB, TB), F32)
            ut = b[rows, ir].T
            b[ir, :] -= jnp.dot(ut, b[rows, :], precision=HI, preferred_element_type=F32)
            return 0

        lax.fori_loop(blk + 1, n, trail, 0)
        return 0

    lax.fori_loop(0, n, step, 0)


def lower_tiles(b):
    ri = lax.broadcasted_iota(jnp.int32, (NB, NB), 0) // TB
    ci = lax.broadcasted_iota(jnp.int32, (NB, NB), 1) // TB
    return jnp.where(ri >= ci, b, 0.0)


def factor_kernel(diag, v0, v1, u01, b0, b1, ud0, ud1, log_det, s11, t, ld):
    ld[...] = jnp.zeros_like(ld)
    b0[...] = diag[0]
    factor_block(b0, t, ud0, ld)
    v0[...] = lower_tiles(b0[...])
    u01[...] = jnp.dot(v0[...], diag[1], precision=HI, preferred_element_type=F32)
    s11[...] = u01[...].T
    b1[...] = diag[2] - jnp.dot(s11[...], u01[...], precision=HI, preferred_element_type=F32)
    factor_block(b1, t, ud1, ld)
    v1[...] = lower_tiles(b1[...])
    log_det[...] = jnp.broadcast_to(jnp.sum(ld[...], axis=0, keepdims=True), (8, 128))


def factor(diag):
    square = jax.ShapeDtypeStruct((NB, NB), F32)
    tiles = jax.ShapeDtypeStruct((NB // TB, TB, TB), F32)
    vmem = pl.BlockSpec(memory_space=pltpu.VMEM)
    return pl.pallas_call(
        factor_kernel,
        name="factor_leading",
        out_shape=(square,) * 5 + (tiles,) * 2 + (jax.ShapeDtypeStruct((8, 128), F32),),
        in_specs=[vmem],
        out_specs=(vmem,) * 8,
        scratch_shapes=[pltpu.VMEM((NB, NB), F32), pltpu.VMEM((TB, 2 * TB), F32), pltpu.VMEM((8, 128), F32)],
        compiler_params=pltpu.CompilerParams(vmem_limit_bytes=60 << 20),
    )(diag)


def mul3(a, b, contract=((1,), (0,))):
    dims = (contract, ((), ()))
    dot = lambda p, q: lax.dot_general(p, q, dims, preferred_element_type=F32)
    return dot(a[0], b[0]) + (dot(a[0], b[1]) + dot(a[1], b[0]))


BT = ((1,), (1,))


def lower_factor(b, ud, out, i0, j0):
    n = NB // TB
    for i in range(n):
        for j in range(n):
            if i > j:
                tile = b[TB * j : TB * j + TB, TB * i : TB * i + TB].T
            elif i == j:
                tile = ud[i].T
            else:
                tile = jnp.zeros((TB, TB), F32)
            out[i0 + TB * i : i0 + TB * i + TB, j0 + TB * j : j0 + TB * j + TB] = tile


def update_kernel(m, arow, acol, v0, v1, u01, b0, b1, ud0, ud1, out, yh, yl, vh, vl, p):
    step = pl.program_id(0)
    row = lax.axis_index("row")
    col = lax.axis_index("col")

    @pl.when(step == 0)
    def _():
        for slot, ref in enumerate((v0, v1, u01)):
            vh[slot], vl[slot] = split2(ref[...])
        for c in range(2):
            cols = pl.ds(c * NB, NB)
            y0 = mul3((vh[0], vl[0]), split2(acol[0, :, cols]))
            y0s = split2(y0)
            yh[:NB, cols], yl[:NB, cols] = y0s
            rest = acol[1, :, cols] - mul3((vh[2], vl[2]), y0s, ((0,), (0,)))
            yh[NB:, cols], yl[NB:, cols] = split2(mul3((vh[1], vl[1]), split2(rest)))

    p0 = mul3(split2(arow[0]), (vh[0], vl[0]), BT)
    p0s = split2(p0)
    rest = arow[1] - mul3(p0s, (vh[2], vl[2]))
    p1 = mul3(split2(rest), (vh[1], vl[1]), BT)
    p1s = split2(p1)
    p[0], p[1] = p0, p1
    for c in range(2):
        cols = pl.ds(c * NB, NB)
        out[:, cols] = m[:, cols] - (
            mul3(p0s, (yh[:NB, cols], yl[:NB, cols])) + mul3(p1s, (yh[NB:, cols], yl[NB:, cols])))

    first = step == 0

    @pl.when(first & (row < 2))
    def _():
        out[...] = jnp.zeros_like(out)

    @pl.when((col == 0) & ~(first & (row == 0)))
    def _():
        out[:, pl.ds(0, NB)] = p[0]

    @pl.when((col == 1) & ~(first & (row < 2)))
    def _():
        out[:, pl.ds(0, NB)] = p[1]

    @pl.when((col == 0) & first & (row == 0))
    def _():
        lower_factor(b0, ud0, out, 0, 0)

    @pl.when((col == 1) & first & (row == 1))
    def _():
        lower_factor(b1, ud1, out, 0, 0)


def update(stored, arow, acol, v0, v1, u01, b0, b1, ud0, ud1):
    rows, cols = stored.shape
    whole = lambda a: pl.BlockSpec(a.shape, lambda i: (0,) * a.ndim, pipeline_mode=pl.Buffered(1))
    return pl.pallas_call(
        update_kernel,
        name="update_remaining",
        grid=(rows // NB,),
        out_shape=jax.ShapeDtypeStruct(stored.shape, F32),
        in_specs=[
            pl.BlockSpec((NB, cols), lambda i: (i, 0)),
            pl.BlockSpec((2, NB, NB), lambda i: (0, i, 0)),
        ]
        + [whole(a) for a in (acol, v0, v1, u01, b0, b1, ud0, ud1)],
        out_specs=pl.BlockSpec((NB, cols), lambda i: (i, 0)),
        scratch_shapes=[
            pltpu.VMEM((2 * NB, cols), BF),
            pltpu.VMEM((2 * NB, cols), BF),
            pltpu.VMEM((3, NB, NB), BF),
            pltpu.VMEM((3, NB, NB), BF),
            pltpu.VMEM((2, NB, NB), F32),
        ],
        compiler_params=pltpu.CompilerParams(vmem_limit_bytes=60 << 20),
    )(stored, arow, acol, v0, v1, u01, b0, b1, ud0, ud1)


def per_device(stored):
    arow, acol, diag = gather(stored)
    v0, v1, u01, b0, b1, ud0, ud1, log_det = factor(diag)
    updated = update(stored, arow, acol, v0, v1, u01, b0, b1, ud0, ud1)
    return updated, log_det[0, 0]


def solution(mesh):
    placed = (P("row", "col"),)
    return jax.shard_map(
        per_device, mesh=mesh, in_specs=placed, out_specs=(P("row", "col"), P()), check_vma=False
    )
```

time: 899 us -> 190 us (0.21); the launches traced: 887 us -> 190 us
  waiting for transfers between devices: 394 us -> 0 us
  other arithmetic: 273 us -> 0 us
  Pallas kernels: 0 us -> 188 us
  local copies, waits for them, and re-layouts: 90.5 us -> 1.2 us
  matrix products: 74.1 us -> 0 us
  blocking collectives: 33 us -> 0 us
  between operations: 21.5 us -> 0.64 us
    psum x4 -> x0, waiting for transfers between devices: 293 us -> none  [from_root_2(): return lax.psum(kept, axis)]
    another operation x35 -> x0, other arithmetic: 241 us -> none  [the longest x29 159 us: per_device(): factor = jnp.linalg.cholesky(pivot_block)]
    pallas_call x0 -> x3, Pallas kernels: none -> 188 us  [the longest x1 109 us: gather(): pl.pallas_call(comm_kernel, name='gather_panels', out_shape=tuple((jax.Sh...]
    all_gather x2 -> x0, waiting for transfers between devices: 100 us -> none  [from_root(): lax.all_gather(value, axis)]
    dot_general x4 -> x0, matrix products: 51.3 us -> none  [the longest x2 34.3 us: per_device(): jnp.dot(left_rows, right_rows.T, precision=lax.Precision.HIGHEST, preferr...]
    psum x1 -> x0, blocking collectives: 33 us -> none  [per_device(): log_total = lax.psum(log_total, 'col')]
    unnamed x32 -> x0, local copies, waits for them, and re-layouts: 31.5 us -> none
    another operation x37 -> x0, local copies, waits for them, and re-layouts: 25.1 us -> none  [the longest x27 23.4 us: per_device(): inverse = jax.scipy.linalg.solve_triangular(factor, identity, lower=True)]
  transfers between devices with their start and end apart: 6 -> 0, of which waited for: 6 -> 0; matrix products, arithmetic and copies ran while one was open for 1% -> 0% of each run, Pallas kernels for 0% -> 0%
where the time goes in v1:
time: 190 us
  Pallas kernels  188 us (99%)
    pallas_call x1, Pallas kernels, gather(): pl.pallas_call(comm_kernel, name='gather_panels', out_shape=tuple((jax.Sh...  109 us
    pallas_call x1, Pallas kernels, factor(): pl.pallas_call(factor_kernel, name='factor_leading', out_shape=(square,)...  43.7 us
    pallas_call x1, Pallas kernels, update(): pl.pallas_call(update_kernel, name='update_remaining', grid=(rows // NB,)...  35.8 us

profile of v1, /device:TPU:64, one launch (start us, length us, event | category | flops | bytes accessed | tf_op | source)
XLA Modules:
  0.0 190.0 jit_solution(7348299390815293046)
XLA Ops:
  0.6 108.7 %gather_panels.1 = (f32[2,2048,512]{2,1,0:T(8,128)}, f32[2,512,1024]{2,1,0:T(8,128)}, f32[3,512,512]{2,1,0:T(8,128)}) custom-call(f32[2048,1024]{1,0:T(8,128)} %m.1), custom_call_target="tpu_custom_call" | custom-call | tf_op jit(solution)/shard_map/gather_panels/pallas_call | solution.py:242
  109.4 43.7 %factor_leading.1 = (f32[512,512]{1,0:T(8,128)}, f32[512,512]{1,0:T(8,128)}, f32[512,512]{1,0:T(8,128)}, f32[512,512]{1,0:T(8,128)}, f32[512,512]{1,0:T(8,128)},...) custom-call(f32[3,512,512]{2,1,0:T(8,128)} %get-tuple-element.15.diag), custom_call_target="tpu_custom_call" | custom-call | tf_op jit(solution)/shard_map/factor_leading/pallas_call | solution.py:378
  153.1 1.2 slice.3
  154.3 35.8 %update_remaining.1 = f32[2048,1024]{1,0:T(8,128)} custom-call(f32[2048,1024]{1,0:T(8,128)} %m.1, f32[2,2048,512]{2,1,0:T(8,128)} %get-tuple-element.13.arow, f32[2,512,1024]{2,1,0:T(8,128)} %get-tuple-element.14.acol, f32[512,512]{1,0:T(8,128)} %get-tuple-element.16.v0, f32[512,512]{1,0:T(8,128)} %get-tuple-element.17.v1, ...), custom_call_target="tpu_custom_call" | custom-call | tf_op jit(solution)/shard_map/update_remaining/pallas_call | solution.py:465

commit v2 on v1

v2 whole, which is shorter than its diff:
```python
import jax
import jax.numpy as jnp
from jax import lax
from jax.experimental import pallas as pl
from jax.experimental.pallas import tpu as pltpu
from jax.sharding import PartitionSpec as P

NB = 512
TB = 128
CH = 32
F32 = jnp.float32
BF = jnp.bfloat16
HI = lax.Precision.HIGHEST
MESH = pl.DeviceIdType.MESH

TREES = (
    (1, 27, 41, 48, 48, 39, 49, 64, 64, 53, 65, 80, 48, 36, 49, 64),
    (2, 48, 64, 48, 23, 40, 58, 46, 35, 50, 66, 50, 48, 64, 80, 64),
    (4, 48, 38, 30, 48, 64, 52, 33, 64, 80, 68, 53, 48, 64, 52, 45),
    (8, 48, 64, 48, 48, 64, 80, 64, 44, 56, 72, 56, 29, 43, 58, 34),
)
MAXDEPTH = 5
SKEW = 3
NX = 16
NQ = 20
D0, D1 = 4, 8
EARLY = 3
DSTEP = 11
LATE = 18
XDELAY = 15
FIRST = 33
SLOW = 6


def lookup(table, position):
    value = jnp.int32(table[0])
    for index in range(1, len(table)):
        value = jnp.where(position == index, jnp.int32(table[index]), value)
    return value


def remote(src, dst, send, recv, device):
    return pltpu.make_async_remote_copy(src, dst, send, recv, device_id=device, device_id_type=MESH)


def panel_kernel(stored, arow_out, acol_out, b_out, u01_out, ud_out, ld_out,
                 buf, other, dx, b, u01, ud, ld, t, s11,
                 lsem, x_recv, xp_recv, x_send, xp_send, p_recv, p_send, d_recv, d_send):
    row = lax.axis_index("row")
    col = lax.axis_index("col")
    x, core = row // 2, row % 2
    z, y = col // 4, col % 4
    partner = (x * 2 + (1 - core), col)
    x_next = (((x + 1) % 4) * 2 + core, col)
    x_prev = (((x + 3) % 4) * 2 + core, col)
    plane = (
        (row, z * 4 + (y + 1) % 4),
        (row, ((z + 1) % 4) * 4 + y),
        (row, z * 4 + (y + 3) % 4),
        (row, ((z + 3) % 4) * 4 + y),
    )
    slab = jnp.where(col < 2, col, 2)
    barrier = pltpu.get_barrier_semaphore()
    for device in (partner, x_next, x_prev) + plane:
        pl.semaphore_signal(barrier, inc=1, device_id=device, device_id_type=MESH)

    @pl.when(x == 0)
    def _():
        own = [
            pltpu.make_async_copy(
                stored.at[pl.ds(0, NB), pl.ds(0, NB)], buf.at[slab, pl.ds(NB, NB), :], lsem.at[0]),
            pltpu.make_async_copy(
                stored.at[pl.ds(0, NB), pl.ds(NB, NB)], buf.at[2, pl.ds(2 * NB, NB), :], lsem.at[1]),
        ]
        for copy in own:
            copy.start()
        own[0].wait()

    for k in range(2):
        @pl.when(col == k)
        def _():
            own = [
                pltpu.make_async_copy(
                    stored.at[pl.ds(0, NB), pl.ds(0, NB)], buf.at[k, pl.ds(0, NB), :], lsem.at[2]),
                pltpu.make_async_copy(
                    stored.at[pl.ds(NB, 3 * NB), pl.ds(0, NB)], buf.at[k, pl.ds(2 * NB, 3 * NB), :], lsem.at[3]),
            ]
            for copy in own:
                copy.start()
            own[0].wait()

    pl.semaphore_wait(barrier, 7)

    def loaded():
        @pl.when(x == 0)
        def _():
            pltpu.make_async_copy(
                stored.at[pl.ds(0, NB), pl.ds(NB, NB)], buf.at[2, pl.ds(2 * NB, NB), :], lsem.at[1]).wait()

        for k in range(2):
            @pl.when(col == k)
            def _():
                pltpu.make_async_copy(
                    stored.at[pl.ds(NB, 3 * NB), pl.ds(0, NB)], buf.at[k, pl.ds(2 * NB, 3 * NB), :], lsem.at[3]).wait()

    def x_rows(d, i):
        return (2 * (i % 8) + d) * CH

    def x_view(d, i):
        second = i // 8
        start = pl.multiple_of(NB + NB * second + x_rows(d, i), CH)
        return buf.at[slab + second * (2 - slab), pl.ds(start, CH), :]

    def x_copy(d, i):
        view = x_view(d, i)
        return remote(view, view, x_send.at[d], x_recv.at[d, i], (x_next, x_prev)[d])

    def xp_copy(d, i):
        target = other.at[i // 8, pl.ds(pl.multiple_of(x_rows(d, i), CH), CH), :]
        return remote(x_view(d, i), target, xp_send.at[d], xp_recv.at[d, i], partner)

    def p_copy(k, t, q, way):
        view = buf.at[k, pl.ds(pl.multiple_of((4 * q + t) * CH, CH), CH), :]
        return remote(view, view, p_send.at[k, t, way], p_recv.at[k, t, q], plane[way])

    def d_copy(k, t, q):
        view = buf.at[k, pl.ds(pl.multiple_of((4 * q + t) * CH, CH), CH), :]
        target = dx.at[k * (1 - core), pl.ds(pl.multiple_of((4 * (q - D0) + t) * CH, CH), CH), :]
        return remote(view, target, d_send.at[k, t], d_recv.at[k, t, q - D0], partner)

    depths, children = [], []
    for k in range(2):
        position = z * 4 + (y + 4 - k) % 4
        codes = [lookup(TREES[t], position) for t in range(4)]
        depths.append([code // 16 for code in codes])
        children.append([[(code // (1 << way)) % 2 == 1 for way in range(4)] for code in codes])
    has_diag = [core == 0, core >= 0]

    def step(s, _):
        for d in range(2):
            distance = x if d == 0 else (4 - x) % 4
            v = s - SKEW * distance - XDELAY * core
            w = s - SLOW * distance - XDELAY * core
            i = jnp.where(v < 8, v, 8 + (w - LATE) // EARLY)
            on_time = (v < 8) | ((w >= LATE) & (w % EARLY == 0))

            @pl.when((v >= 0) & (i < NX) & on_time)
            def _():
                @pl.when(distance > 0)
                def _():
                    x_copy(d, i).wait_recv()

                @pl.when(i > 0)
                def _():
                    xp_copy(d, i - 1).wait_send()

                xp_copy(d, i).start()

                @pl.when(distance < 3)
                def _():
                    @pl.when(i > 0)
                    def _():
                        x_copy(d, i - 1).wait_send()

                    x_copy(d, i).start()

        for k in range(2):
            for t in range(4):
                v = s - SKEW * depths[k][t]
                late = s - SLOW * depths[k][t]
                w = (late - LATE) // EARLY
                q_late = 8 + w
                if k == 1:
                    q_late = q_late - core * jnp.where(w < 3, 0, jnp.where(w < 7, 7, 4))
                q = jnp.where(v < DSTEP, v // EARLY, jnp.where(v < LATE, D0 + (v - DSTEP) // 2, q_late))
                early = (v >= 0) & (v < EARLY * D0) & (v % EARLY == 0)
                diag = (v >= DSTEP) & (v < LATE) & ((v - DSTEP) % 2 == 0) & (core == 0)
                active = early | diag | ((late >= LATE) & (late % EARLY == 0) & (q < NQ))
                in_diag = (q >= D0) & (q < D1)

                @pl.when(active)
                def _():
                    @pl.when(depths[k][t] > 0)
                    def _():
                        p_copy(k, t, q, 0).wait_recv()

                    for way in range(4):
                        @pl.when(children[k][t][way])
                        def _():
                            @pl.when(q > 0)
                            def _():
                                p_copy(k, t, q - 1, way).wait_send()

                            p_copy(k, t, q, way).start()

                    @pl.when(in_diag)
                    def _():
                        @pl.when(q > D0)
                        def _():
                            d_copy(k, t, q - 1).wait_send()

                        d_copy(k, t, q).start()
        return 0

    def take(k):
        for t in range(4):
            for j in range(D1 - D0):
                d_copy(k, t, D0 + j).wait_recv()

    lax.fori_loop(0, 12, step, 0)
    loaded()
    lax.fori_loop(12, FIRST, step, 0)

    ri = lax.broadcasted_iota(jnp.int32, (TB, TB), 0)
    ci = lax.broadcasted_iota(jnp.int32, (TB, TB), 1)
    n = NB // TB
    ld[...] = jnp.zeros_like(ld)

    @pl.when(core == 0)
    def _():
        b[0] = buf[0, pl.ds(NB, NB), :]

    @pl.when(core == 1)
    def _():
        take(0)
        b[0] = dx[0]

    def tile(g, _):
        half, blk = g // n, g % n

        @pl.when(g == n)
        def _():
            v0 = lower_tiles(b[0])

            @pl.when(core == 0)
            def _():
                take(1)
                u01[...] = jnp.dot(v0, buf[1, pl.ds(NB, NB), :], precision=HI, preferred_element_type=F32)
                b[1] = dx[0]

            @pl.when(core == 1)
            def _():
                take(1)
                u01[...] = jnp.dot(v0, dx[1], precision=HI, preferred_element_type=F32)
                b[1] = buf[1, pl.ds(NB, NB), :]

            s11[...] = u01[...].T
            b[1] -= jnp.dot(s11[...], u01[...], precision=HI, preferred_element_type=F32)

        base = pl.multiple_of(blk * TB, TB)
        rows = pl.ds(base, TB)
        t[:, :TB] = b[half, rows, rows]
        t[:, TB:] = jnp.where(ri == ci, 1.0, 0.0)
        begin = jnp.where(g < n, 3 * g, n + 2 * g)
        finish = begin + jnp.where((g < n) | (g == 2 * n - 1), 3, 2)

        def late_step(u, _):
            return step(FIRST + EARLY * u, 0)

        factor_tile(t, ld, lambda: late_step(begin, 0))
        w = jnp.where(ri >= ci, t[:, TB:], 0.0)
        ud[g] = jnp.where(ri <= ci, t[:, :TB], 0.0)
        b[half, rows, :] = mul6(split3(w), split3(b[half, rows, :]))
        b[half, rows, rows] = w
        done = b[half, rows, :]
        change = mul6(split3(done.T), split3(done))
        for i in range(1, n):
            @pl.when(blk < i)
            def _():
                b[half, TB * i : TB * i + TB, rows] = jnp.zeros((TB, TB), F32)
                b[half, TB * i : TB * i + TB, :] -= change[TB * i : TB * i + TB, :]

        lax.fori_loop(begin + 1, finish, late_step, 0)
        return 0

    lax.fori_loop(0, 2 * n, tile, 0)

    for d in range(2):
        distance = x if d == 0 else (4 - x) % 4
        xp_copy(d, NX - 1).wait_send()
        for i in range(NX):
            xp_copy(d, i).wait_recv()

        @pl.when(distance < 3)
        def _():
            x_copy(d, NX - 1).wait_send()
    for k in range(2):
        for t in range(4):
            for way in range(4):
                @pl.when(children[k][t][way])
                def _():
                    p_copy(k, t, NQ - 1, way).wait_send()

            @pl.when(has_diag[k])
            def _():
                d_copy(k, t, D1 - 1).wait_send()

    first, second = pl.ds(0, NB), pl.ds(NB, NB)
    outs = [
        (buf.at[pl.ds(0, 2), first, :], arow_out.at[:, first, :]),
        (buf.at[pl.ds(0, 2), pl.ds(2 * NB, 3 * NB), :], arow_out.at[:, pl.ds(NB, 3 * NB), :]),
        (buf.at[slab, second, :], acol_out.at[core, :, first]),
        (buf.at[2, pl.ds(2 * NB, NB), :], acol_out.at[core, :, second]),
        (other.at[0], acol_out.at[1 - core, :, first]),
        (other.at[1], acol_out.at[1 - core, :, second]),
        (u01, u01_out),
        (ud, ud_out),
        (b, b_out),
        (ld, ld_out),
    ]
    copies = [pltpu.make_async_copy(src, dst, lsem.at[index]) for index, (src, dst) in enumerate(outs)]
    for copy in copies:
        copy.start()
    for copy in copies:
        copy.wait()


def panels(stored):
    rows, cols = stored.shape
    n = NB // TB
    outs = ((2, rows, NB), (2, NB, cols), (2, NB, NB), (NB, NB), (2 * n, TB, TB), (8, 128))
    scratch = ((3, rows + NB, NB), (2, NB, NB), (2, NB, NB), (2, NB, NB), (NB, NB), (2 * n, TB, TB), (8, 128),
               (TB, 2 * TB), (NB, NB))
    dma = pltpu.SemaphoreType.DMA
    return pl.pallas_call(
        panel_kernel,
        name="gather_and_factor",
        out_shape=tuple(jax.ShapeDtypeStruct(s, F32) for s in outs),
        in_specs=[pl.BlockSpec(memory_space=pl.ANY)],
        out_specs=(pl.BlockSpec(memory_space=pl.ANY),) * len(outs),
        scratch_shapes=[pltpu.VMEM(s, F32) for s in scratch]
        + [
            dma((10,)),
            dma((2, NX)),
            dma((2, NX)),
            dma((2,)),
            dma((2,)),
            dma((2, 4, NQ)),
            dma((2, 4, 4)),
            dma((2, 4, D1 - D0)),
            dma((2, 4)),
        ],
        compiler_params=pltpu.CompilerParams(
            collective_id=0, has_side_effects=True, vmem_limit_bytes=60 << 20),
    )(stored)


def spread(value, k):
    return jnp.broadcast_to(value[k : k + 1, :], (8, 128))


def split3(value):
    high = value.astype(BF)
    rest = value - high.astype(F32)
    middle = rest.astype(BF)
    low = (rest - middle.astype(F32)).astype(BF)
    return high, middle, low


def split2(value):
    high = value.astype(BF)
    return high, (value - high.astype(F32)).astype(BF)


def mul6(a, b):
    lhs = jnp.concatenate([a[0], a[0], a[1], a[0], a[2], a[1]], 1)
    rhs = jnp.concatenate([b[0], b[1], b[0], b[2], b[0], b[1]], 0)
    return jnp.dot(lhs, rhs, preferred_element_type=F32)


def factor_tile(t, ld, between):
    sub = lax.broadcasted_iota(jnp.int32, (8, 128), 0)
    for p in range(8):
        r0 = 16 * p
        r = [[t[r0 + 8 * g : r0 + 8 * g + 8, 128 * h : 128 * h + 128] for h in range(2)] for g in range(2)]
        top = [jnp.broadcast_to(r[0][0][:, r0 + j : r0 + j + 1], (8, 128)) for j in range(8)]
        bot = [jnp.broadcast_to(r[1][0][:, r0 + j : r0 + j + 1], (8, 128)) for j in range(16)]
        piv = [jnp.ones((8, 128), F32), jnp.ones((8, 128), F32)]
        for k in range(16):
            g, kk = divmod(k, 8)
            pv = spread(top[k] if g == 0 else bot[k], kk)
            inv = 1.0 / pv
            piv[g] = jnp.where(sub == kk, pv, piv[g])
            mb = bot[k] * inv
            mt = top[k] * inv if g == 0 else None
            for j in range(k + 1, 16):
                s = spread(top[k], j) if j < 8 else spread(bot[k], j - 8)
                bot[j] = bot[j] - mb * s
                if j < 8:
                    top[j] = top[j] - mt * s
            for h in range(2):
                u = spread(r[g][h], kk)
                if g == 0:
                    r[0][h] = r[0][h] - jnp.where(sub > kk, mt, 0.0) * u
                    r[1][h] = r[1][h] - mb * u
                else:
                    r[1][h] = r[1][h] - jnp.where(sub > kk, mb, 0.0) * u
        ld[...] += jnp.log(piv[0]) + jnp.log(piv[1])
        rows = []
        for g in range(2):
            rs = lax.rsqrt(piv[g])
            rows.append([r[g][h] * rs for h in range(2)])
            for h in range(2):
                t[r0 + 8 * g : r0 + 8 * g + 8, 128 * h : 128 * h + 128] = rows[g][h]
        if p < 7:
            uh, um, ul = split3(jnp.concatenate([rows[0][0], rows[1][0]], 0))
            wh, wm, wl = split3(jnp.concatenate([rows[0][1], rows[1][1]], 0))
            lhs = jnp.concatenate([uh, uh, um, uh, ul, um], 0)
            rhs = jnp.concatenate(
                [jnp.concatenate([uh, um, uh, ul, uh, um], 0), jnp.concatenate([wh, wm, wh, wl, wh, wm], 0)], 1)
            upd = lax.dot_general(lhs, rhs, (((0,), (0,)), ((), ())), preferred_element_type=F32)
            t[r0 + 16 :, :] -= upd[r0 + 16 :, :]
        if p == 3:
            between()


def lower_tiles(b):
    ri = lax.broadcasted_iota(jnp.int32, (NB, NB), 0) // TB
    ci = lax.broadcasted_iota(jnp.int32, (NB, NB), 1) // TB
    return jnp.where(ri >= ci, b, 0.0)


def mul3(a, b, contract=((1,), (0,))):
    dims = (contract, ((), ()))
    dot = lambda p, q: lax.dot_general(p, q, dims, preferred_element_type=F32)
    return dot(a[0], b[0]) + (dot(a[0], b[1]) + dot(a[1], b[0]))


BT = ((1,), (1,))


def lower_factor(k, b, ud, out):
    n = NB // TB
    for i in range(n):
        for j in range(n):
            if i > j:
                tile = b[k, TB * j : TB * j + TB, TB * i : TB * i + TB].T
            elif i == j:
                tile = ud[k * n + i].T
            else:
                tile = jnp.zeros((TB, TB), F32)
            out[TB * i : TB * i + TB, TB * j : TB * j + TB] = tile


def update_kernel(m, arow, acol, b, u01, ud, ld, out, log_det, yh, yl, vh, vl, p):
    step = pl.program_id(0)
    row = lax.axis_index("row")
    col = lax.axis_index("col")

    @pl.when(step == 0)
    def _():
        log_det[0, 0] = jnp.sum(ld[:, 0:1])
        for slot in range(2):
            vh[slot], vl[slot] = split2(lower_tiles(b[slot]))
        vh[2], vl[2] = split2(u01[...])
        for c in range(2):
            cols = pl.ds(c * NB, NB)
            y0 = mul3((vh[0], vl[0]), split2(acol[0, :, cols]))
            y0s = split2(y0)
            yh[:NB, cols], yl[:NB, cols] = y0s
            rest = acol[1, :, cols] - mul3((vh[2], vl[2]), y0s, ((0,), (0,)))
            yh[NB:, cols], yl[NB:, cols] = split2(mul3((vh[1], vl[1]), split2(rest)))

    p0 = mul3(split2(arow[0]), (vh[0], vl[0]), BT)
    p0s = split2(p0)
    rest = arow[1] - mul3(p0s, (vh[2], vl[2]))
    p1 = mul3(split2(rest), (vh[1], vl[1]), BT)
    p1s = split2(p1)
    p[0], p[1] = p0, p1
    for c in range(2):
        cols = pl.ds(c * NB, NB)
        out[:, cols] = m[:, cols] - (
            mul3(p0s, (yh[:NB, cols], yl[:NB, cols])) + mul3(p1s, (yh[NB:, cols], yl[NB:, cols])))

    first = step == 0

    @pl.when(first & (row < 2))
    def _():
        out[...] = jnp.zeros_like(out)

    @pl.when((col == 0) & ~(first & (row == 0)))
    def _():
        out[:, pl.ds(0, NB)] = p[0]

    @pl.when((col == 1) & ~(first & (row < 2)))
    def _():
        out[:, pl.ds(0, NB)] = p[1]

    @pl.when((col == 0) & first & (row == 0))
    def _():
        lower_factor(0, b, ud, out)

    @pl.when((col == 1) & first & (row == 1))
    def _():
        lower_factor(1, b, ud, out)


def update(stored, arow, acol, b, u01, ud, ld):
    rows, cols = stored.shape
    whole = lambda a: pl.BlockSpec(a.shape, lambda i: (0,) * a.ndim, pipeline_mode=pl.Buffered(1))
    return pl.pallas_call(
        update_kernel,
        name="update_remaining",
        grid=(rows // NB,),
        out_shape=(jax.ShapeDtypeStruct(stored.shape, F32), jax.ShapeDtypeStruct((1, 1), F32)),
        in_specs=[
            pl.BlockSpec((NB, cols), lambda i: (i, 0)),
            pl.BlockSpec((2, NB, NB), lambda i: (0, i, 0)),
        ]
        + [whole(a) for a in (acol, b, u01, ud, ld)],
        out_specs=(pl.BlockSpec((NB, cols), lambda i: (i, 0)), pl.BlockSpec(memory_space=pltpu.SMEM)),
        scratch_shapes=[
            pltpu.VMEM((2 * NB, cols), BF),
            pltpu.VMEM((2 * NB, cols), BF),
            pltpu.VMEM((3, NB, NB), BF),
            pltpu.VMEM((3, NB, NB), BF),
            pltpu.VMEM((2, NB, NB), F32),
        ],
        compiler_params=pltpu.CompilerParams(vmem_limit_bytes=60 << 20),
    )(stored, arow, acol, b, u01, ud, ld)


def per_device(stored):
    updated, log_det = update(stored, *panels(stored))
    return updated, log_det.reshape(())


def solution(mesh):
    placed = (P("row", "col"),)
    return jax.shard_map(
        per_device, mesh=mesh, in_specs=placed, out_specs=(P("row", "col"), P()), check_vma=False
    )
```

time: 190 us -> 158 us (0.83)
  Pallas kernels: 188 us -> 156 us
    pallas_call x2 -> x1, Pallas kernels: 152 us -> 121 us  [panels(): pl.pallas_call(panel_kernel, name='gather_and_factor', out_shape=tuple((j...]
where the time goes in v2:
time: 158 us; the launch traced here: 157 us
  Pallas kernels  156 us (99%)
    pallas_call x1, Pallas kernels, panels(): pl.pallas_call(panel_kernel, name='gather_and_factor', out_shape=tuple((j...  121 us
    pallas_call x1, Pallas kernels, update(): pl.pallas_call(update_kernel, name='update_remaining', grid=(rows // NB,)...  35.5 us

profile of v2, /device:TPU:64, one launch (start us, length us, event | category | flops | bytes accessed | tf_op | source)
XLA Modules:
  0.0 157.0 jit_solution(2039397679672767858)
XLA Ops:
  0.6 120.9 %gather_and_factor.1 = (f32[2,2048,512]{2,1,0:T(8,128)}, f32[2,512,1024]{2,1,0:T(8,128)}, f32[2,512,512]{2,1,0:T(8,128)}, f32[512,512]{1,0:T(8,128)}, f32[8,128,128]{2,1,0:T(8,128)}, /*index=5*/f32[8,128]{1,0:T(8,128)}) custom-call(f32[2048,1024]{1,0:T(8,128)} %m.1), custom_call_target="tpu_custom_call" | custom-call | tf_op jit(solution)/shard_map/gather_and_factor/pallas_call | solution.py:325
  121.5 35.5 %update_remaining.1 = (f32[2048,1024]{1,0:T(8,128)}, f32[1,1]{1,0:T(1,128)}) custom-call(f32[2048,1024]{1,0:T(8,128)} %m.1, f32[2,2048,512]{2,1,0:T(8,128)} %get-tuple-element.10.arow, f32[2,512,1024]{2,1,0:T(8,128)} %get-tuple-element.11.acol, f32[2,512,512]{2,1,0:T(8,128)} %get-tuple-element.12.b, f32[512,512]{1,0:T(8,128)} %get-tuple-element.13.u01, ...), custom_call_target="tpu_custom_call" | custom-call | tf_op jit(solution)/shard_map/update_remaining/pallas_call | solution.py:501

commit v3 on v2

--- a/solution.py
+++ b/solution.py
@@ -447,6 +447,20 @@
     row = lax.axis_index("row")
     col = lax.axis_index("col")
 
+    half = NB // 2
+
+    def times_lower(slot, a):
+        short = [part[:, :half] for part in a]
+        return jnp.concatenate([
+            mul3(short, (vh[slot, :half, :half], vl[slot, :half, :half]), BT),
+            mul3(a, (vh[slot, half:, :], vl[slot, half:, :]), BT)], 1)
+
+    def lower_times(slot, a):
+        short = [part[:half] for part in a]
+        return jnp.concatenate([
+            mul3((vh[slot, :half, :half], vl[slot, :half, :half]), short),
+            mul3((vh[slot, half:, :], vl[slot, half:, :]), a)], 0)
+
     @pl.when(step == 0)
     def _():
         log_det[0, 0] = jnp.sum(ld[:, 0:1])
@@ -455,16 +469,16 @@
         vh[2], vl[2] = split2(u01[...])
         for c in range(2):
             cols = pl.ds(c * NB, NB)
-            y0 = mul3((vh[0], vl[0]), split2(acol[0, :, cols]))
+            y0 = lower_times(0, split2(acol[0, :, cols]))
             y0s = split2(y0)
             yh[:NB, cols], yl[:NB, cols] = y0s
             rest = acol[1, :, cols] - mul3((vh[2], vl[2]), y0s, ((0,), (0,)))
-            yh[NB:, cols], yl[NB:, cols] = split2(mul3((vh[1], vl[1]), split2(rest)))
-
-    p0 = mul3(split2(arow[0]), (vh[0], vl[0]), BT)
+            yh[NB:, cols], yl[NB:, cols] = split2(lower_times(1, split2(rest)))
+
+    p0 = times_lower(0, split2(arow[0]))
     p0s = split2(p0)
     rest = arow[1] - mul3(p0s, (vh[2], vl[2]))
-    p1 = mul3(split2(rest), (vh[1], vl[1]), BT)
+    p1 = times_lower(1, split2(rest))
     p1s = split2(p1)
     p[0], p[1] = p0, p1
     for c in range(2):

time: 158 us -> 160 us (1.013)
  Pallas kernels: 156 us -> 159 us
    pallas_call x1, Pallas kernels: 35.5 us -> 37.7 us  [update(): pl.pallas_call(update_kernel, name='update_remaining', grid=(rows // NB,)...]
where the time goes in v3:
time: 160 us; the launch traced here: 159 us
  Pallas kernels  159 us (99%)
    pallas_call x1, Pallas kernels, panels(): pl.pallas_call(panel_kernel, name='gather_and_factor', out_shape=tuple((j...  121 us
    pallas_call x1, Pallas kernels, update(): pl.pallas_call(update_kernel, name='update_remaining', grid=(rows // NB,)...  37.7 us

profile of v3, /device:TPU:64, one launch (start us, length us, event | category | flops | bytes accessed | tf_op | source)
XLA Modules:
  0.0 159.2 jit_solution(10028929423253466565)
XLA Ops:
  0.6 120.9 %gather_and_factor.1 = (f32[2,2048,512]{2,1,0:T(8,128)}, f32[2,512,1024]{2,1,0:T(8,128)}, f32[2,512,512]{2,1,0:T(8,128)}, f32[512,512]{1,0:T(8,128)}, f32[8,128,128]{2,1,0:T(8,128)}, /*index=5*/f32[8,128]{1,0:T(8,128)}) custom-call(f32[2048,1024]{1,0:T(8,128)} %m.1), custom_call_target="tpu_custom_call" | custom-call | tf_op jit(solution)/shard_map/gather_and_factor/pallas_call | solution.py:325
  121.5 37.7 %update_remaining.1 = (f32[2048,1024]{1,0:T(8,128)}, f32[1,1]{1,0:T(1,128)}) custom-call(f32[2048,1024]{1,0:T(8,128)} %m.1, f32[2,2048,512]{2,1,0:T(8,128)} %get-tuple-element.10.arow, f32[2,512,1024]{2,1,0:T(8,128)} %get-tuple-element.11.acol, f32[2,512,512]{2,1,0:T(8,128)} %get-tuple-element.12.b, f32[512,512]{1,0:T(8,128)} %get-tuple-element.13.u01, ...), custom_call_target="tpu_custom_call" | custom-call | tf_op jit(solution)/shard_map/update_remaining/pallas_call | solution.py:515
